TPU v7x, 32 devices: a whole 2x2x4 slice. The times are simulated.
32 devices in a mesh: gx: 4 (over x, core), gy: 8 (over z, y).
Axes of the slice: x: 2, y: 2, z: 4, core: 2. Of those that a mesh axis runs over, the one named last changes fastest.
Arguments:
- slot_tiles: int32 [32, 32], P(('gx', 'gy')), may hold values from -1 to 63, as said below
- owner_map: int32 [32], replicated, may hold values from 0 to 31, each once
- slot_depth: int32 [32, 32, 16, 128], P(('gx', 'gy')), may hold values from 0 to 1073741823
- slot_color: bfloat16 [32, 32, 16, 3, 128], P(('gx', 'gy')), may hold values from 0 to 1
Outputs:
- region_depth: int32 [32, 2, 16, 128], P(('gx', 'gy'))
- region_color: bfloat16 [32, 2, 16, 3, 128], P(('gx', 'gy'))
- thumbnail: float32 [32, 3, 64], replicated
Inputs may be any that keep to these rules, and one draw needn't show every extreme that they name: `slot_tiles`: each rank's used slots name the tiles of one rectangle of at least 4 tile rows of the 8 x 8 tile grid, each once, in row-major order, followed by -1 in the unused slots; all ranks' rectangles contain a common region. `owner_map`: each rank owns exactly one region.
All inputs are finite; a program needn't handle non-finite values.
Results may differ from a plain program's by a relative error of at most 0.001.
Values may be sent and summed in bfloat16 or wider, within the bound.
A program may use at most 64 MiB of HBM per device.

v0:
```python
import jax
import jax.numpy as jnp
from jax import lax
from jax.sharding import PartitionSpec as P

far_depth = 1073741824


def composite(pieces):
    depth_stack, color_stack = pieces
    nearest = jnp.min(depth_stack, axis=0)
    winner = jnp.argmin(depth_stack, axis=0)
    stack_index = lax.broadcasted_iota(jnp.int32, depth_stack.shape, 0)
    chosen = jnp.expand_dims(stack_index == winner[None], -2)
    masked = jnp.where(chosen, color_stack, jnp.zeros((), color_stack.dtype))
    picked = jnp.max(masked, axis=0)
    return (nearest, picked)


def pack_tiles(slot_tiles, owner_map, slot_depth, slot_color):
    grid_rows = lax.axis_size("gx")
    grid_cols = lax.axis_size("gy")
    region_count = grid_rows * grid_cols
    slot_count = slot_tiles.shape[1]
    tile_ids = slot_tiles[0]
    is_live = tile_ids >= 0
    safe_tile = jnp.where(is_live, tile_ids, 0)
    tile_row = safe_tile // grid_cols
    tile_col = safe_tile % grid_cols
    tile_region = tile_row // 2 * grid_cols + tile_col
    tile_half = tile_row % 2
    owner_rank = owner_map[tile_region]
    position = owner_rank * 2 + tile_half
    position = jnp.where(is_live, position, 2 * region_count)
    source_slot = jnp.full((2 * region_count + 1,), slot_count, jnp.int32)
    source_slot = source_slot.at[position].set(jnp.arange(slot_count, dtype=jnp.int32))[
        : 2 * region_count
    ]
    has_slot = source_slot < slot_count
    safe_slot = jnp.minimum(source_slot, slot_count - 1)
    rows_depth = jnp.take(slot_depth[0], safe_slot, axis=0)
    rows_color = jnp.take(slot_color[0], safe_slot, axis=0)
    send_depth = jnp.where(has_slot[:, None, None], rows_depth, far_depth)
    send_color = jnp.where(has_slot[:, None, None, None], rows_color, jnp.zeros((), jnp.bfloat16))
    return (send_depth, send_color)


def shards(slot_tiles, owner_map, slot_depth, slot_color):
    grid_rows = lax.axis_size("gx")
    grid_cols = lax.axis_size("gy")
    band_rows = slot_depth.shape[2]
    tile_width = slot_depth.shape[3]
    send_depth, send_color = pack_tiles(slot_tiles, owner_map, slot_depth, slot_color)
    send_depth = send_depth.reshape(grid_rows * grid_cols, 2, band_rows, tile_width)
    send_color = send_color.reshape(grid_rows * grid_cols, 2, band_rows, 3, tile_width)
    merged_depth, merged_color = composite(
        (
            lax.all_to_all(send_depth, ("gx", "gy"), split_axis=0, concat_axis=0, tiled=True),
            lax.all_to_all(send_color, ("gx", "gy"), split_axis=0, concat_axis=0, tiled=True),
        )
    )
    block_means = (
        merged_color.astype(jnp.float32)
        .reshape(2, band_rows // 8, 8, 3, tile_width // 8, 8)
        .mean(axis=(2, 5))
    )
    thumb_rows = jnp.transpose(block_means, (2, 0, 1, 3)).reshape(3, -1)
    gathered = lax.all_gather(thumb_rows[None], ("gx", "gy"), axis=0, tiled=True)
    thumbnail = gathered[owner_map]
    return (merged_depth[None], merged_color[None], thumbnail)


def solution(mesh):
    placed = (
        P(("gx", "gy"), None),
        P(),
        P(("gx", "gy"), None, None, None),
        P(("gx", "gy"), None, None, None, None),
    )
    return jax.shard_map(
        shards,
        mesh=mesh,
        in_specs=placed,
        out_specs=(P(("gx", "gy"), None, None, None), P(("gx", "gy"), None, None, None, None), P()),
        check_vma=False,
    )
```

profile of v0, /device:TPU:0, one launch (start us, length us, event | category | flops | bytes accessed | tf_op | source)
XLA Modules:
  0.0 120.9 jit_solution(16057108061104475037)
XLA Ops:
  0.6 0.0 copy-start
  0.6 0.7 fusion.2
  1.4 0.0 copy-start.1
  1.4 0.6 copy-done.1
  2.0 0.0 copy-start.2
  2.0 0.7 gather_fusion
  2.7 0.7 copy-done.4
  3.4 0.7 scatter_custom_fusion
  4.1 0.1 lt.72
  4.2 0.1 min.14
  4.4 0.0 copy-done.2
  4.4 0.6 gather_fusion.1
  5.0 1.0 select_select_fusion.1
  6.0 7.3 %all-to-all-start = ((s32[32,2,16,128]{3,2,1,0:T(8,128)}), s32[32,2,16,128]{3,2,1,0:T(8,128)S(1)}, u32[]{:S(2)}, u32[]{:S(2)}) async-start(s32[32,2,16,128]{3,2,1,0:T(8,128)} %select_select_fusion.1), calls=%async_computation | async-start | bytes 1048576 | tf_op jit(solution)/shard_map/all_to_all | solution.py:58
  13.4 0.0 copy-done
  13.4 0.7 gather_fusion.2
  14.1 1.1 select_select_fusion
  15.2 14.4 %all-to-all-done = s32[32,2,16,128]{3,2,1,0:T(8,128)S(1)} async-done(((s32[32,2,16,128]{3,2,1,0:T(8,128)}), s32[32,2,16,128]{3,2,1,0:T(8,128)S(1)}, u32[]{:S(2)}, u32[]{:S(2)}) %all-to-all-start) | async-done | bytes 524320 | tf_op jit(solution)/shard_map/all_to_all | solution.py:58
  29.6 2.6 %all-to-all-start.1 = ((bf16[32,2,16,3,128]{4,2,3,1,0:T(8,128)(2,1)}), bf16[32,2,16,3,128]{4,2,3,1,0:T(8,128)(2,1)S(1)}, u32[]{:S(2)}, u32[]{:S(2)}) async-start(bf16[32,2,16,3,128]{4,2,3,1,0:T(8,128)(2,1)} %select_select_fusion), calls=%async_computation.1 | async-start | bytes 1572864 | tf_op jit(solution)/shard_map/all_to_all | solution.py:59
  32.2 0.7 reduce_min.9
  32.9 0.7 iota_reduce_fusion
  33.6 0.1 iota_compare_fusion
  33.7 20.4 %all-to-all-done.1 = bf16[32,2,16,3,128]{4,2,3,1,0:T(8,128)(2,1)S(1)} async-done(((bf16[32,2,16,3,128]{4,2,3,1,0:T(8,128)(2,1)}), bf16[32,2,16,3,128]{4,2,3,1,0:T(8,128)(2,1)S(1)}, u32[]{:S(2)}, u32[]{:S(2)}) %all-to-all-start.1) | async-done | bytes 786464 | tf_op jit(solution)/shard_map/all_to_all | solution.py:59
  54.1 0.3 select_reduce_fusion
  54.3 0.0 copy-start.3
  54.4 0.4 reshape.232
  54.8 0.2 copy-done.3
  55.0 0.1 reduce_sum.9
  55.1 0.1 broadcast_in_dim_reshape.3
  55.2 64.4 %all_gather.3 = f32[32,3,64]{2,1,0:T(4,128)S(1)} all-gather(f32[1,3,64]{2,1,0:T(4,128)S(1)} %broadcast_in_dim_reshape.3), channel_id=1, replica_groups=mesh['gx'=4,'gy'=8] {'gx','gy'}, dimensions={0}, use_global_device_ids=true | all-gather | bytes 25344 | tf_op jit(solution)/shard_map/all_gather | solution.py:68
  119.7 0.6 gather_fusion.3
  120.3 0.6 copy.9
  (12 shorter events, 0.1 us)
Async XLA Ops:
  0.6 12.7 %copy-start = (bf16[1,32,16,3,128]{4,2,3,1,0:T(8,128)(2,1)S(1)}, bf16[1,32,16,3,128]{4,2,3,1,0:T(8,128)(2,1)}, u32[]{:S(2)}) copy-start(bf16[1,32,16,3,128]{4,2,3,1,0:T(8,128)(2,1)} %param.7) | copy-start | bytes 1179652
  1.4 0.7 copy-start.1
  2.0 2.3 %copy-start.2 = (s32[1,32,16,128]{3,2,1,0:T(8,128)S(1)}, s32[1,32,16,128]{3,2,1,0:T(8,128)}, u32[]{:S(2)}) copy-start(s32[1,32,16,128]{3,2,1,0:T(8,128)} %param.6) | copy-start | bytes 786436
  2.7 0.7 copy-start.4
  6.0 23.6 %all-to-all-start = ((s32[32,2,16,128]{3,2,1,0:T(8,128)}), s32[32,2,16,128]{3,2,1,0:T(8,128)S(1)}, u32[]{:S(2)}, u32[]{:S(2)}) async-start(s32[32,2,16,128]{3,2,1,0:T(8,128)} %select_select_fusion.1), calls=%async_computation | async-start | bytes 1048576 | tf_op jit(solution)/shard_map/all_to_all | solution.py:58
  29.6 24.5 %all-to-all-start.1 = ((bf16[32,2,16,3,128]{4,2,3,1,0:T(8,128)(2,1)}), bf16[32,2,16,3,128]{4,2,3,1,0:T(8,128)(2,1)S(1)}, u32[]{:S(2)}, u32[]{:S(2)}) async-start(bf16[32,2,16,3,128]{4,2,3,1,0:T(8,128)(2,1)} %select_select_fusion), calls=%async_computation.1 | async-start | bytes 1572864 | tf_op jit(solution)/shard_map/all_to_all | solution.py:59
  54.3 0.6 copy-start.3
where the time goes:
time: 121 us
  blocking collectives  64.4 us (53%)
  waiting for transfers between devices  34.8 us (29%)
  starting transfers between devices  9.95 us (8%)
  local copies, waits for them, and re-layouts  6.13 us (5%)
  other arithmetic  4.73 us (4%)
    all_gather x1, blocking collectives, shards(): lax.all_gather(thumb_rows[None], ('gx', 'gy'), axis=0, tiled=True)  64.4 us
    all_to_all x1, waiting for transfers between devices, shards(): lax.all_to_all(send_color, ('gx', 'gy'), split_axis=0, concat_axis=0, til...  20.4 us
    all_to_all x1, waiting for transfers between devices, shards(): lax.all_to_all(send_depth, ('gx', 'gy'), split_axis=0, concat_axis=0, til...  14.4 us
    all_to_all x1, starting transfers between devices, shards(): lax.all_to_all(send_depth, ('gx', 'gy'), split_axis=0, concat_axis=0, til...  7.33 us
    all_to_all x1, starting transfers between devices, shards(): lax.all_to_all(send_color, ('gx', 'gy'), split_axis=0, concat_axis=0, til...  2.62 us
  transfers between devices with their start and end apart: 2, of which 2 were waited for; matrix products, arithmetic and copies ran while one was open for 3% of the time, Pallas kernels for 0%

commit v1 on v0

v1 whole, which is shorter than its diff:
```python
import functools

import jax
import jax.numpy as jnp
from jax import lax
from jax.experimental import pallas as pl
from jax.experimental.pallas import tpu as pltpu
from jax.sharding import PartitionSpec as P

FAR = 1073741824
HALF = 536870912
LOWEST = -2147483648
MESH = pl.DeviceIdType.MESH


def div_const(value, by):
    if by & (by - 1) == 0:
        return value >> (by.bit_length() - 1)
    return value // by


def merge(first, second):
    key_a, colors_a = first
    key_b, colors_b = second
    nearer = key_b < key_a
    key = jnp.where(nearer, key_b, key_a)
    return key, [jnp.where(nearer, b, a) for a, b in zip(colors_a, colors_b)]


def kernel(
    dims, inv_ref, own_ref, slots_ref, depth_ref, color_ref,
    out_d, out_c, out_t,
    cs_d, cs_c, cr_d, cr_c, ys_d, ys_c, yr_d, yr_c, zs_d, zs_c, zr_d, zr_c, xs_d, xs_c, xr_d, xr_c,
    gath,
    c_ss, c_rs, y_ss, y_rs, z_ss, z_rs, x_ss, x_rs, g1_ss, g1_rs, g2_ss, g2_rs,
):
    GX, GY, X, Y, Z = dims
    regions = GX * GY
    gx = lax.axis_index("gx")
    gy = lax.axis_index("gy")
    core = lax.rem(gx, 2)
    x = lax.div(gx, 2)
    y = lax.rem(gy, Y)
    z = lax.div(gy, Y)
    tile_cols = GY

    barrier = pltpu.get_barrier_semaphore()
    for j in range(1, GX):
        pl.semaphore_signal(barrier, inc=1, device_id=(lax.rem(gx + j, GX), gy), device_id_type=MESH)
    for j in range(1, GY):
        pl.semaphore_signal(barrier, inc=1, device_id=(gx, lax.rem(gy + j, GY)), device_id_type=MESH)

    first = slots_ref[0, 0]
    last = first
    for s in range(1, slots_ref.shape[1]):
        last = jnp.maximum(last, slots_ref[0, s])
    top = div_const(first, tile_cols)
    left = first - top * tile_cols
    bottom = div_const(last, tile_cols)
    right = last - bottom * tile_cols
    width = right - left + 1

    def own_tile(owner_core, owner_x, owner_y, owner_z, half):
        rank = (owner_x * 2 + owner_core) * GY + owner_z * Y + owner_y
        region = inv_ref[rank]
        pair = div_const(region, tile_cols)
        col = region - pair * tile_cols
        row = pair * 2 + half
        live = (row >= top) & (row <= bottom) & (col >= left) & (col <= right)
        slot = jnp.where(live, (row - top) * width + (col - left), 0)
        floor = jnp.where(live, LOWEST, 2 * HALF)
        key = jnp.maximum((depth_ref[slot] - HALF) * 2, floor) + core
        return key, [color_ref[slot, c] for c in range(3)]

    def load(ref_d, ref_c, index):
        return ref_d[index], [ref_c[index + (c,)] for c in range(3)]

    def store(ref_d, ref_c, index, value):
        ref_d[index] = value[0]
        for c in range(3):
            ref_c[index + (c,)] = value[1][c]

    pending = []

    def remote(src, dst, ss, rs, device):
        return pltpu.make_async_remote_copy(
            src_ref=src, dst_ref=dst, send_sem=ss, recv_sem=rs, device_id=device, device_id_type=MESH
        )

    def send(pairs, sems, device):
        for k, (src, dst) in enumerate(pairs):
            copy = remote(src, dst, sems[0].at[sems[1] + (k,)], sems[2].at[sems[3] + (k,)], device)
            copy.start()
            pending.append(copy)

    def arrived(refs, rs, index, device):
        for k, ref in enumerate(refs):
            remote(ref, ref, c_ss.at[0, k], rs.at[index + (k,)], device).wait_recv()

    other_core = 1 - core
    core_partner = (x * 2 + other_core, gy)
    me = (gx, gy)
    chunk_x = [lax.rem(x + 1 + j, X) for j in range(X)]

    for j in range(X):

        def pack(i, carry, j=j):
            yy = lax.div(i, Z)
            zz = lax.rem(i, Z)
            for h in range(2):
                store(cs_d, cs_c, (j, yy, zz, h), own_tile(other_core, chunk_x[j], yy, zz, h))
            return carry

        lax.fori_loop(0, Y * Z, pack, 0)
        if j == 0:
            pl.semaphore_wait(barrier, GX + GY - 2)
        send([(cs_d.at[j], cr_d.at[j]), (cs_c.at[j], cr_c.at[j])], (c_ss, (j,), c_rs, (j,)), core_partner)

    lane_k = lax.broadcasted_iota(jnp.int32, (128, 128), 0) // 8
    lane_l = lax.broadcasted_iota(jnp.int32, (128, 128), 1)
    groups = []
    for h in range(2):
        hit = (lane_l == lane_k + 32 * h) | (lane_l == lane_k + 32 * h + 80)
        groups.append(jnp.where(hit, 1.0 / 64.0, 0.0).astype(jnp.bfloat16))

    for j in range(X):
        arrived([cr_d.at[j], cr_c.at[j]], c_rs, (j,), me)
        for i in range(Y):
            yy = lax.rem(y + 1 + i, Y)
            mine = i == Y - 1

            def step(zz, carry, j=j, yy=yy, mine=mine):
                for h in range(2):
                    value = merge(
                        own_tile(core, chunk_x[j], yy, zz, h), load(cr_d, cr_c, (j, yy, zz, h))
                    )
                    if mine:
                        store(yr_d, yr_c, (j, y, zz, h), value)
                    else:
                        store(ys_d, ys_c, (j, yy, zz, h), value)
                return carry

            lax.fori_loop(0, Z, step, 0)
            if not mine:
                send(
                    [(ys_d.at[j, yy], yr_d.at[j, y]), (ys_c.at[j, yy], yr_c.at[j, y])],
                    (y_ss, (j, i), y_rs, (j, y)),
                    (gx, z * Y + yy),
                )

    for j in range(X):
        for i in range(Y - 1):
            yy = lax.rem(y + 1 + i, Y)
            arrived([yr_d.at[j, yy], yr_c.at[j, yy]], y_rs, (j, yy), me)
        for i in range(Z):
            zz = lax.rem(z + 1 + i, Z)
            mine = i == Z - 1
            for h in range(2):
                value = load(yr_d, yr_c, (j, 0, zz, h))
                for k in range(1, Y):
                    value = merge(value, load(yr_d, yr_c, (j, k, zz, h)))
                if mine:
                    store(zr_d, zr_c, (j, z, h), value)
                else:
                    store(zs_d, zs_c, (j, zz, h), value)
            if not mine:
                send(
                    [(zs_d.at[j, zz], zr_d.at[j, z]), (zs_c.at[j, zz], zr_c.at[j, z])],
                    (z_ss, (j, i), z_rs, (j, z)),
                    (gx, zz * Y + y),
                )

    for j in range(X):
        for i in range(Z - 1):
            zz = lax.rem(z + 1 + i, Z)
            arrived([zr_d.at[j, zz], zr_c.at[j, zz]], z_rs, (j, zz), me)
        mine = j == X - 1
        for h in range(2):
            value = load(zr_d, zr_c, (j, 0, h))
            for k in range(1, Z):
                value = merge(value, load(zr_d, zr_c, (j, k, h)))
            value = (value[0] >> 1, value[1])
            if mine:
                store(xr_d, xr_c, (x, h), value)
            else:
                store(xs_d, xs_c, (j, h), value)
        if not mine:
            send(
                [(xs_d.at[j], xr_d.at[x]), (xs_c.at[j], xr_c.at[x])],
                (x_ss, (j,), x_rs, (x,)),
                (chunk_x[j] * 2 + core, gy),
            )

    for j in range(X - 1):
        xx = chunk_x[j]
        arrived([xr_d.at[xx], xr_c.at[xx]], x_rs, (xx,), me)

    sums = [None] * 3
    row = lax.broadcasted_iota(jnp.int32, (16, 128), 0)
    lane = lax.broadcasted_iota(jnp.int32, (16, 128), 1)
    keep = (row < 8) == (lane < 64)
    for h in range(2):
        value = load(xr_d, xr_c, (0, h))
        for k in range(1, X):
            value = merge(value, load(xr_d, xr_c, (k, h)))
        depth = value[0] + HALF
        out_d[h] = depth
        for c in range(3):
            color = jnp.where(depth == FAR, jnp.zeros((), jnp.bfloat16), value[1][c])
            out_c[h, c] = color
            part = jnp.dot(color, groups[h], preferred_element_type=jnp.float32)
            part = jnp.where(keep, part, 0.0)
            sums[c] = part if sums[c] is None else sums[c] + part
    rows = []
    for c in range(3):
        total = jnp.sum(sums[c], axis=0, keepdims=True)
        rows.append(total + pltpu.roll(total, 64, 1))
    lane_row = lax.broadcasted_iota(jnp.int32, (1, 128), 1)
    gath[gy, gx, 0:1, :] = jnp.where(lane_row < 64, rows[0], rows[1])
    gath[gy, gx, 1:2, :] = rows[2]

    for j in range(1, GX):
        send([(gath.at[gy, gx], gath.at[gy, gx])], (g1_ss, (j,), g1_rs, (gx,)), (lax.rem(gx + j, GX), gy))
    for j in range(1, GX):
        xx = lax.rem(gx + j, GX)
        arrived([gath.at[gy, xx]], g1_rs, (xx,), me)
    for j in range(1, GY):
        send([(gath.at[gy], gath.at[gy])], (g2_ss, (j,), g2_rs, (gy,)), (gx, lax.rem(gy + j, GY)))
    for j in range(1, GY):
        yy = lax.rem(gy + j, GY)
        arrived([gath.at[yy]], g2_rs, (yy,), me)

    def place(r, carry):
        owner = own_ref[r]
        owner_x = div_const(owner, GY)
        out_t[r] = gath[owner - owner_x * GY, owner_x]
        return carry

    lax.fori_loop(0, regions, place, 0)
    for copy in pending:
        copy.wait_send()


def shards(slot_tiles, owner_map, slot_depth, slot_color):
    GX = lax.axis_size("gx")
    GY = lax.axis_size("gy")
    X, Z = GX // 2, 4
    Y = GY // Z
    regions = GX * GY
    band, width = slot_depth.shape[2:]
    ids = jnp.arange(regions, dtype=jnp.int32)
    inverse = jnp.sum(jnp.where(owner_map[None, :] == ids[:, None], ids[None, :], 0), axis=1)
    depth = slot_depth[0]
    color = jnp.transpose(slot_color[0], (0, 2, 1, 3))

    def pair(*lead):
        return [
            pltpu.VMEM(lead + (2, band, width), jnp.int32),
            pltpu.VMEM(lead + (2, 3, band, width), jnp.bfloat16),
        ]

    dma = lambda *shape: pltpu.SemaphoreType.DMA(shape)
    vmem = pl.BlockSpec(memory_space=pltpu.VMEM)
    smem = pl.BlockSpec(memory_space=pltpu.SMEM)
    out_d, out_c, out_t = pl.pallas_call(
        functools.partial(kernel, (GX, GY, X, Y, Z)),
        out_shape=(
            jax.ShapeDtypeStruct((2, band, width), jnp.int32),
            jax.ShapeDtypeStruct((2, 3, band, width), jnp.bfloat16),
            jax.ShapeDtypeStruct((regions, 2, width), jnp.float32),
        ),
        in_specs=[smem, smem, smem, vmem, vmem],
        out_specs=(vmem, vmem, vmem),
        scratch_shapes=[
            *pair(X, Y, Z), *pair(X, Y, Z),
            *pair(X, Y, Z), *pair(X, Y, Z),
            *pair(X, Z), *pair(X, Z),
            *pair(X), *pair(X),
            pltpu.VMEM((GY, GX, 2, width), jnp.float32),
            dma(X, 2), dma(X, 2),
            dma(X, Y, 2), dma(X, Y, 2),
            dma(X, Z, 2), dma(X, Z, 2),
            dma(X, 2), dma(X, 2),
            dma(GX, 1), dma(GX, 1),
            dma(GY, 1), dma(GY, 1),
        ],
        compiler_params=pltpu.CompilerParams(collective_id=0, has_side_effects=True),
    )(inverse, owner_map, slot_tiles, depth, color)
    thumbnail = out_t.reshape(regions, 2 * width)[:, : 3 * width // 2].reshape(regions, 3, width // 2)
    return (out_d[None], jnp.transpose(out_c, (0, 2, 1, 3))[None], thumbnail)


def solution(mesh):
    placed = (
        P(("gx", "gy"), None),
        P(),
        P(("gx", "gy"), None, None, None),
        P(("gx", "gy"), None, None, None, None),
    )
    return jax.shard_map(
        shards,
        mesh=mesh,
        in_specs=placed,
        out_specs=(P(("gx", "gy"), None, None, None), P(("gx", "gy"), None, None, None, None), P()),
        check_vma=False,
    )
```

time: 121 us -> 37.4 us (0.31)
  blocking collectives: 64.4 us -> 0 us
  waiting for transfers between devices: 34.8 us -> 0 us
  Pallas kernels: 0 us -> 32.2 us
  starting transfers between devices: 9.95 us -> 0 us
  other arithmetic: 4.73 us -> 0.63 us
  local copies, waits for them, and re-layouts: 6.13 us -> 3.56 us
    all_gather x1 -> x0, blocking collectives: 64.4 us -> none  [shards(): lax.all_gather(thumb_rows[None], ('gx', 'gy'), axis=0, tiled=True)]
    all_to_all x2 -> x0, waiting for transfers between devices: 34.8 us -> none  [the longest x1 20.4 us: shards(): lax.all_to_all(send_color, ('gx', 'gy'), split_axis=0, concat_axis=0, til...]
    pallas_call x0 -> x1, Pallas kernels: none -> 32.2 us  [shards(): pl.pallas_call(functools.partial(kernel, (GX, GY, X, Y, Z)), out_shape=(j...]
    all_to_all x2 -> x0, starting transfers between devices: 9.95 us -> none  [the longest x1 7.33 us: shards(): lax.all_to_all(send_depth, ('gx', 'gy'), split_axis=0, concat_axis=0, til...]
    select_n x5 -> x0, other arithmetic: 2.83 us -> none  [the longest x1 1.08 us: pack_tiles(): jnp.where(has_slot[:, None, None, None], rows_color, jnp.zeros((), jnp.bf...]
    gather x4 -> x0, local copies, waits for them, and re-layouts: 2.64 us -> none  [the longest x1 0.7 us: pack_tiles(): rows_color = jnp.take(slot_color[0], safe_slot, axis=0)]
    unnamed x11 -> x10, local copies, waits for them, and re-layouts: 2.11 us -> 3.47 us
  transfers between devices with their start and end apart: 2 -> 0, of which waited for: 2 -> 0; matrix products, arithmetic and copies ran while one was open for 3% -> 0% of each run, Pallas kernels for 0% -> 0%
where the time goes in v1:
time: 37.4 us; the launch traced here: 37.1 us
  Pallas kernels  32.2 us (86%)
  local copies, waits for them, and re-layouts  3.56 us (10%)
  between operations  0.66 us (2%)
  other arithmetic  0.63 us (2%)
    pallas_call x1, Pallas kernels, shards(): pl.pallas_call(functools.partial(kernel, (GX, GY, X, Y, Z)), out_shape=(j...  32.2 us
    unnamed x10, local copies, waits for them, and re-layouts  3.47 us

profile of v1, /device:TPU:0, one launch (start us, length us, event | category | flops | bytes accessed | tf_op | source)
XLA Modules:
  0.0 37.1 jit_solution(14408394110718443632)
XLA Ops:
  0.6 0.0 copy-start.2
  0.6 0.6 %copy-done.2 = s32[32]{0:T(128)S(1)} copy-done((s32[32]{0:T(128)S(1)}, s32[32]{0:T(128)}, u32[]{:S(2)}) %copy-start.2) | copy-done | bytes 152
  1.3 0.6 %select_reduce_fusion.inv_ref = s32[32]{0:T(128)} fusion(s32[32]{0:T(128)S(1)} %copy-done.2), kind=kLoop, calls=%fused_computation.1 | loop fusion | flops 3040 | bytes 256 | tf_op jit(solution)/shard_map/reduce_sum | solution.py:252
  1.9 32.2 %shard_map.67 = (s32[2,16,128]{2,1,0:T(8,128)}, bf16[2,3,16,128]{3,2,1,0:T(8,128)(2,1)}, f32[32,2,128]{2,1,0:T(2,128)}) custom-call(s32[32]{0:T(128)} %select_reduce_fusion.inv_ref, s32[32]{0:T(128)} %own_ref.1, s32[1,32]{1,0:T(1,128)} %slots_ref.1, s32[32,16,128]{2,1,0:T(8,128)} %bitcast.14, bf16[32,3,16,128]{3,2,1,0:T(8,128)(2,1)} %bitcast.13), custom_call_target="tpu_custom_call" | custom-call | tf_op jit(solution)/shard_map/pallas_call | solution.py:265
  34.1 0.8 %copy.11 = f32[4,8,2,128]{3,1,2,0:T(8,128)S(1)} copy(f32[4,8,2,128]{3,2,1,0:T(2,128)} %bitcast.16) | data formatting | bytes 65536
  34.9 0.1 reshape.14
  35.0 0.0 copy-start.1
  35.0 0.6 %copy.8 = f32[32,3,64]{2,0,1:T(8,128)} copy(f32[32,3,64]{2,1,0:T(4,128)S(1)} %reshape.14) | data formatting | bytes 49152
  35.6 0.1 copy-done.1
  35.7 0.0 copy-start
  35.7 0.6 %copy.14 = s32[1,2,16,128]{3,2,1,0:T(8,128)} copy(s32[1,2,16,128]{3,2,1,0:T(8,128)S(1)} %bitcast.18) | data formatting | bytes 32768
  36.3 0.1 copy-done
  36.5 0.6 %copy.15 = bf16[1,2,16,3,128]{4,2,3,1,0:T(8,128)(2,1)} copy(bf16[1,2,16,3,128]{4,2,3,1,0:T(8,128)(2,1)S(1)} %bitcast.17) | data formatting | bytes 49152
Async XLA Ops:
  0.6 0.7 %copy-start.2 = (s32[32]{0:T(128)S(1)}, s32[32]{0:T(128)}, u32[]{:S(2)}) copy-start(s32[32]{0:T(128)} %own_ref.1) | copy-start | bytes 388
  35.0 0.7 %copy-start.1 = (s32[2,16,128]{2,1,0:T(8,128)S(1)}, s32[2,16,128]{2,1,0:T(8,128)}, u32[]{:S(2)}) copy-start(s32[2,16,128]{2,1,0:T(8,128)} %get-tuple-element.6) | copy-start | bytes 49156
  35.7 0.7 %copy-start = (bf16[2,3,16,128]{3,2,1,0:T(8,128)(2,1)S(1)}, bf16[2,3,16,128]{3,2,1,0:T(8,128)(2,1)}, u32[]{:S(2)}) copy-start(bf16[2,3,16,128]{3,2,1,0:T(8,128)(2,1)} %get-tuple-element.7) | copy-start | bytes 73732

commit v2 on v1

--- a/solution.py
+++ b/solution.py
@@ -239,6 +239,16 @@
     lax.fori_loop(0, regions, place, 0)
     for copy in pending:
         copy.wait_send()
+
+
+def finish(in_d, in_c, in_t, out_d, out_c, out_t):
+    out_d[...] = in_d[...]
+    out_c[...] = in_c[...]
+    side = out_t.shape[2]
+    upper = in_t[:, 0, :]
+    out_t[0] = upper[:, :side]
+    out_t[1] = upper[:, side:]
+    out_t[2] = in_t[:, 1, :][:, :side]
 
 
 def shards(slot_tiles, owner_map, slot_depth, slot_color):
@@ -286,7 +296,17 @@
         ],
         compiler_params=pltpu.CompilerParams(collective_id=0, has_side_effects=True),
     )(inverse, owner_map, slot_tiles, depth, color)
-    thumbnail = out_t.reshape(regions, 2 * width)[:, : 3 * width // 2].reshape(regions, 3, width // 2)
+    out_d, out_c, out_t = pl.pallas_call(
+        finish,
+        out_shape=(
+            jax.ShapeDtypeStruct((2, band, width), jnp.int32),
+            jax.ShapeDtypeStruct((2, 3, band, width), jnp.bfloat16),
+            jax.ShapeDtypeStruct((3, regions, width // 2), jnp.float32),
+        ),
+        in_specs=[vmem, vmem, vmem],
+        out_specs=(vmem, vmem, vmem),
+    )(out_d, out_c, out_t)
+    thumbnail = jnp.transpose(out_t, (1, 0, 2))
     return (out_d[None], jnp.transpose(out_c, (0, 2, 1, 3))[None], thumbnail)
 
 

time: 37.4 us -> 35.9 us (0.960)
  local copies, waits for them, and re-layouts: 3.56 us -> 0.65 us
  Pallas kernels: 32.2 us -> 33.7 us
    unnamed x10 -> x2, local copies, waits for them, and re-layouts: 3.47 us -> 0.65 us
    pallas_call x0 -> x1, Pallas kernels: none -> 1.5 us  [shards(): pl.pallas_call(finish, out_shape=(jax.ShapeDtypeStruct((2, band, width),...]
where the time goes in v2:
time: 35.9 us; the launch traced here: 35.6 us
  Pallas kernels  33.7 us (94%)
  local copies, waits for them, and re-layouts  0.65 us (2%)
  between operations  0.65 us (2%)
  other arithmetic  0.63 us (2%)
    pallas_call x1, Pallas kernels, shards(): pl.pallas_call(functools.partial(kernel, (GX, GY, X, Y, Z)), out_shape=(j...  32.2 us
    pallas_call x1, Pallas kernels, shards(): pl.pallas_call(finish, out_shape=(jax.ShapeDtypeStruct((2, band, width),...  1.5 us

profile of v2, /device:TPU:0, one launch (start us, length us, event | category | flops | bytes accessed | tf_op | source)
XLA Modules:
  0.0 35.6 jit_solution(5996222867138461521)
XLA Ops:
  0.6 0.0 copy-start
  0.6 0.6 %copy-done = s32[32]{0:T(128)S(1)} copy-done((s32[32]{0:T(128)S(1)}, s32[32]{0:T(128)}, u32[]{:S(2)}) %copy-start) | copy-done | bytes 152
  1.3 0.6 %select_reduce_fusion.inv_ref = s32[32]{0:T(128)} fusion(s32[32]{0:T(128)S(1)} %copy-done), kind=kLoop, calls=%fused_computation | loop fusion | flops 3040 | bytes 256 | tf_op jit(solution)/shard_map/reduce_sum | solution.py:262
  1.9 32.2 %shard_map.67 = (s32[2,16,128]{2,1,0:T(8,128)}, bf16[2,3,16,128]{3,2,1,0:T(8,128)(2,1)}, f32[32,2,128]{2,1,0:T(2,128)}) custom-call(s32[32]{0:T(128)} %select_reduce_fusion.inv_ref, s32[32]{0:T(128)} %own_ref.1, s32[1,32]{1,0:T(1,128)} %slots_ref.1, s32[32,16,128]{2,1,0:T(8,128)} %bitcast.10, bf16[32,3,16,128]{3,2,1,0:T(8,128)(2,1)} %bitcast.9), custom_call_target="tpu_custom_call" | custom-call | tf_op jit(solution)/shard_map/pallas_call | solution.py:275
  34.1 1.5 %shard_map.68 = (s32[2,16,128]{2,1,0:T(8,128)}, bf16[2,3,16,128]{3,2,1,0:T(8,128)(2,1)}, f32[3,32,64]{2,1,0:T(8,128)}) custom-call(s32[2,16,128]{2,1,0:T(8,128)} %get-tuple-element.9.in_d, bf16[2,3,16,128]{3,2,1,0:T(8,128)(2,1)} %get-tuple-element.10.in_c, f32[32,2,128]{2,1,0:T(2,128)} %get-tuple-element.11.in_t), custom_call_target="tpu_custom_call" | custom-call | tf_op jit(solution)/shard_map/pallas_call | solution.py:299
Async XLA Ops:
  0.6 0.7 %copy-start = (s32[32]{0:T(128)S(1)}, s32[32]{0:T(128)}, u32[]{:S(2)}) copy-start(s32[32]{0:T(128)} %own_ref.1) | copy-start | bytes 388
